TPU v7x, 512 devices: a whole 4x4x16 slice. The times are simulated.
512 devices in a mesh: seq: 64 (over z, y), head: 8 (over x, core).
Axes of the slice: x: 4, y: 4, z: 16, core: 2. Of those that a mesh axis runs over, the one named last changes fastest.
Arguments:
- queries: bfloat16 [8192, 16, 128], P('seq', 'head'), may hold values from -6 to 6
- key_vectors: bfloat16 [8192, 16, 128], P('seq', 'head'), may hold values from -16 to 16
- values: bfloat16 [8192, 16, 128], P('seq', 'head'), may hold values from -6 to 6
- out_gate: bfloat16 [8192, 16, 128], P('seq', 'head'), may hold values from -6 to 6
- inputs: bfloat16 [8192, 2048], P('seq', 'head'), may hold values from -6 to 6
- beta_weight: bfloat16 [16, 2048], P(None, 'head'), may hold values from -0.1875 to 0.1875
- log_decay: float32 [16, 8192], P('head', 'seq'), may hold values from -1 to 0
- initial_state: float32 [16, 128, 128], P('head'), may hold values from -6 to 6
Outputs:
- gated_out: bfloat16 [8192, 16, 128], P('seq', 'head')
- block_states: float32 [128, 16, 128, 128], P('seq', 'head')
All inputs are finite; a program needn't handle non-finite values.
Results may differ from a plain program's by a relative error of at most 0.0012.
Values sent between devices are 32-bit elements; how exact they have to be, the bound alone decides.
A program may use at most 64 MiB of HBM per device.

v0:
```python
import jax
import jax.numpy as jnp
from jax import lax
from jax.sharding import Mesh
from jax.sharding import PartitionSpec as P

BLOCK = 64
SEQ = ("seq_0", "seq_1")


EPSILON = 1e-06


def nothing_yet(array, identity):
    return jax.tree.map(
        lambda a, e: jnp.broadcast_to(jnp.asarray(e, a.dtype), a.shape), array, identity
    )


def entering(array, axes, combine, identity):
    before = start = nothing_yet(array, identity)
    so_far = array
    for axis in reversed(axes):
        length, place = (lax.axis_size(axis), lax.axis_index(axis))
        pieces = jax.tree.map(lambda part: lax.all_gather(part, axis), so_far)
        inside, so_far = (start, start)
        for k in range(length):
            passed = k < place
            so_far = combine(so_far, jax.tree.map(lambda part: part[k], pieces))
            inside = jax.tree.map(lambda new, old: jnp.where(passed, new, old), so_far, inside)
        before = combine(inside, before)
    return before


def split_up(array, dim, length):
    dims = array.shape
    tiles = array.reshape(*dims[:dim], length, dims[dim] // length, *dims[dim + 1 :])
    return jnp.moveaxis(tiles, dim, 0)


def sent_and_summed(array, axis, dim):
    tiles = split_up(array, dim, lax.axis_size(axis))
    arrived = lax.all_to_all(tiles, axis, split_axis=0, concat_axis=0, tiled=True)
    return arrived.sum(axis=0)


def from_everyone(array, axis):
    copies = jnp.broadcast_to(array, (lax.axis_size(axis), *array.shape))
    return lax.all_to_all(copies, axis, split_axis=0, concat_axis=0, tiled=True)


def of_everyone(array, axis):
    return from_everyone(array, axis).sum(axis=0)


def matmul(matrix, operand):
    return jnp.einsum("...ij,...jk->...ik", matrix, operand, precision=lax.Precision.HIGHEST)


def normalize(query_block, key_block, key_limit):
    query_float = query_block.astype(jnp.float32)
    key_float = key_block.astype(jnp.float32)
    queries_unit = (
        query_float
        / jnp.sqrt(jnp.sum(query_float * query_float, -1, keepdims=True) + EPSILON)
        * query_float.shape[-1] ** (-0.5)
    )
    keys_unit = key_float / jnp.maximum(
        jnp.sqrt(jnp.sum(key_float * key_float, -1, keepdims=True)), key_limit
    )
    return (queries_unit, keys_unit)


def block_parts(queries_unit, keys_unit, value_rows, beta_gate, decay_rows):
    length = decay_rows.shape[-1]
    feature = keys_unit.shape[-1]
    cumulative = jnp.cumsum(decay_rows, axis=-1)
    inside = jnp.tril(jnp.ones((length, length), jnp.float32))
    strict = jnp.tril(jnp.ones((length, length), jnp.float32), -1)
    spread = jnp.where(inside > 0, cumulative[..., :, None] - cumulative[..., None, :], 0.0)
    damping = jnp.exp(spread) * inside
    intersections = jnp.einsum(
        "...id,...jd->...ij", keys_unit, keys_unit, precision=lax.Precision.HIGHEST
    )
    system = (
        jnp.eye(length, dtype=jnp.float32)
        + beta_gate[..., :, None] * intersections * damping * strict
    )
    right_side = jnp.concatenate(
        [
            (beta_gate * jnp.exp(cumulative))[..., None] * keys_unit,
            beta_gate[..., None] * value_rows,
        ],
        axis=-1,
    )
    solved = lax.linalg.triangular_solve(
        system, right_side, left_side=True, lower=True, unit_diagonal=True
    )
    write_keys = solved[..., :feature]
    write_values = solved[..., feature:]
    final_sum = cumulative[..., -1:]
    carried = keys_unit * jnp.exp(final_sum - cumulative)[..., None]
    transition = jnp.exp(final_sum)[..., None] * jnp.eye(feature, dtype=jnp.float32) - jnp.einsum(
        "...ld,...le->...de", carried, write_keys, precision=lax.Precision.HIGHEST
    )
    offset = jnp.einsum(
        "...ld,...le->...de", carried, write_values, precision=lax.Precision.HIGHEST
    )
    reached = queries_unit * jnp.exp(cumulative)[..., None]
    scores = (
        jnp.einsum("...id,...jd->...ij", queries_unit, keys_unit, precision=lax.Precision.HIGHEST)
        * damping
    )
    return (write_keys, write_values, transition, offset, reached, scores)


def block_out(block_info, state_now):
    write_keys, write_values, transition, offset, reached, scores = block_info
    corrected = write_values - matmul(write_keys, state_now)
    return matmul(reached, state_now) + matmul(scores, corrected)


def gate_norm(raw_out, gate_rows):
    inverse_rms = 1.0 / jnp.sqrt(jnp.mean(raw_out * raw_out, -1, keepdims=True) + EPSILON)
    return (raw_out * inverse_rms * jax.nn.silu(gate_rows.astype(jnp.float32))).astype(jnp.bfloat16)


def combine(earlier, latter):
    return (matmul(latter[0], earlier[0]), matmul(latter[0], earlier[1]) + latter[1])


def advance(queries_unit, keys_unit, value_rows, beta_gate, decay_rows, start_state):
    block_info = block_parts(queries_unit, keys_unit, value_rows, beta_gate, decay_rows)
    transition = jnp.moveaxis(block_info[2], 1, 0)
    offset = jnp.moveaxis(block_info[3], 1, 0)
    head_count = transition.shape[1]
    feature = transition.shape[2]
    identity_map = jnp.broadcast_to(
        jnp.eye(feature, dtype=jnp.float32), (head_count, feature, feature)
    )
    zero_state = jnp.zeros((head_count, feature, value_rows.shape[-1]), jnp.float32)

    def compose(carried_map, block_map):
        return (
            (
                matmul(block_map[0], carried_map[0]),
                matmul(block_map[0], carried_map[1]) + block_map[1],
            ),
            carried_map,
        )

    (device_map, device_offset), prefixes = lax.scan(
        compose, (identity_map, zero_state), (transition, offset)
    )
    before_map, before_offset = entering(
        (device_map, device_offset), SEQ, combine, (identity_map, zero_state)
    )
    entry_state = matmul(before_map, start_state) + before_offset
    starts = matmul(prefixes[0], entry_state[None]) + prefixes[1]
    raw_out = block_out(block_info, jnp.moveaxis(starts, 0, 1))
    return (raw_out, starts)


def on_device(
    queries, key_vectors, values, out_gate, inputs, beta_weight, log_decay, initial_state
):
    token_count, head_count, feature = queries.shape
    blocks = token_count // BLOCK
    logits = sent_and_summed(
        lax.dot_general(
            beta_weight, inputs, (((1,), (1,)), ((), ())), preferred_element_type=jnp.float32
        ),
        "head",
        0,
    )
    beta_gate = jax.nn.sigmoid(logits)
    key_float = key_vectors.astype(jnp.float32)
    key_total = of_everyone(jnp.sum(key_float * key_float, axis=(0, 2)), SEQ)
    key_limit = jnp.sqrt(key_total / (token_count * lax.axis_size(SEQ)) + EPSILON)
    queries_unit, keys_unit = normalize(queries, key_vectors, key_limit[:, None])

    def arrange(tensor):
        return tensor.reshape(blocks, BLOCK, head_count, -1).transpose(2, 0, 1, 3)

    query_blocks = arrange(queries_unit)
    key_blocks = arrange(keys_unit)
    value_blocks = arrange(values.astype(jnp.float32))
    beta_blocks = beta_gate.reshape(head_count, blocks, BLOCK)
    decay_blocks = log_decay.reshape(head_count, blocks, BLOCK)
    raw_out, starts = advance(
        query_blocks, key_blocks, value_blocks, beta_blocks, decay_blocks, initial_state
    )
    gated_out = gate_norm(
        raw_out.transpose(1, 2, 0, 3).reshape(token_count, head_count, feature), out_gate
    )
    return (gated_out, starts)


def solution(mesh):
    finer = Mesh(mesh.devices.reshape(16, 4, mesh.shape["head"]), ("seq_0", "seq_1", "head"))
    in_specs = (
        P(SEQ, "head", None),
        P(SEQ, "head", None),
        P(SEQ, "head", None),
        P(SEQ, "head", None),
        P(SEQ, "head"),
        P(None, "head"),
        P("head", SEQ),
        P("head", None, None),
    )
    out_specs = (P(SEQ, "head", None), P(SEQ, "head", None, None))
    return jax.shard_map(
        on_device, mesh=finer, in_specs=in_specs, out_specs=out_specs, check_vma=False
    )
```

profile of v0, /device:TPU:6, one launch (start us, length us, event | category | flops | bytes accessed | tf_op | source)
XLA Modules:
  0.0 243.8 jit_solution(7677255935314597026)
XLA Ops:
  7.2 1.2 fusion.28
  9.0 18.7 %all-to-all-start = ((f32[64,1,2]{2,1,0:T(1,128)}), f32[64,1,2]{2,1,0:T(1,128)S(1)}, u32[]{:S(2)}, u32[]{:S(2)}) async-start(f32[64,1,2]{2,1,0:T(1,128)} %broadcast_in_dim.57), calls=%async_computation | async-start | bytes 65536 | tf_op jit(solution)/shard_map/all_to_all | solution.py:49
  29.2 1.6 fusion.84
  31.8 10.5 %all-to-all-done = f32[64,1,2]{2,1,0:T(1,128)S(1)} async-done(((f32[64,1,2]{2,1,0:T(1,128)}), f32[64,1,2]{2,1,0:T(1,128)S(1)}, u32[]{:S(2)}, u32[]{:S(2)}) %all-to-all-start) | async-done | bytes 544 | tf_op jit(solution)/shard_map/all_to_all | solution.py:49
  42.3 4.8 %all-to-all-start.1 = ((f32[8,2,128]{2,1,0:T(2,128)}), f32[8,2,128]{2,1,0:T(2,128)S(1)}, u32[]{:S(2)}, u32[]{:S(2)}) async-start(f32[8,2,128]{2,1,0:T(2,128)} %bitcast.5), calls=%async_computation.1 | async-start | bytes 16384 | tf_op jit(solution)/shard_map/all_to_all | solution.py:43
  47.2 1.0 convert_divide_fusion
  48.3 2.0 all-to-all-done.1
  50.9 19.7 %custom-call.3 = f32[2,2,1,64,64]{3,4,2,1,0:T(8,128)S(1)} custom-call(f32[2,2,1,64,64]{4,3,2,1,0:T(8,128)S(1)} %fusion.21), custom_call_target="InvertDiagBlocksLowerTriangular" | custom-call | tf_op jit(solution)/shard_map/triangular_solve | solution.py:96
  72.5 1.6 while.17
  74.1 13.6 %all-gather = f32[8,128,128]{2,1,0:T(8,128)S(1)} all-gather(f32[2,128,128]{2,1,0:T(8,128)S(1)} %get-tuple-element.42), channel_id=2, replica_groups=mesh['seq_0'=16,'seq_1'=4,'head'=8] {'seq_1'}, dimensions={0}, use_global_device_ids=true | all-gather | bytes 655360 | tf_op jit(solution)/shard_map/all_gather | solution.py:25
  88.5 0.9 fusion.91
  90.4 13.4 %all-gather.2 = f32[8,128,128]{2,1,0:T(8,128)S(1)} all-gather(f32[2,128,128]{2,1,0:T(8,128)S(1)} %get-tuple-element.43), channel_id=4, replica_groups=mesh['seq_0'=16,'seq_1'=4,'head'=8] {'seq_1'}, dimensions={0}, use_global_device_ids=true | all-gather | bytes 655360 | tf_op jit(solution)/shard_map/all_gather | solution.py:25
  104.6 0.9 convolution_add_fusion.16
  105.9 45.9 %all-gather.7.cloned.1.call-done = f32[32,128,128]{2,1,0:T(8,128)} async-done(((f32[2,128,128]{2,1,0:T(8,128)}), f32[32,128,128]{2,1,0:T(8,128)}) %all-gather.7.cloned.1.call-update) | async-done | bytes 2097168 | tf_op jit(solution)/shard_map/all_gather | solution.py:25
  151.7 1.3 fusion.60
  153.1 1.2 fusion.92
  154.2 1.2 fusion.93
  155.4 1.2 fusion.94
  160.2 63.7 %all-gather.9.cloned.1.call-done = f32[32,128,128]{2,1,0:T(8,128)} async-done(((f32[2,128,128]{2,1,0:T(8,128)}), f32[32,128,128]{2,1,0:T(8,128)}) %all-gather.9.cloned.1.call-update) | async-done | bytes 2097168 | tf_op jit(solution)/shard_map/all_gather | solution.py:25
  223.9 1.3 convolution_add_fusion.20
  225.2 1.2 convolution_add_fusion.15
  226.4 1.2 convolution_add_fusion.14
  227.6 1.2 convolution_add_fusion.13
  236.0 0.9 fusion.47
  (115 shorter events, 20.4 us)
Async XLA Ops:
  7.2 225.2 %copy-start = (f32[2,128,128]{2,1,0:T(8,128)S(1)}, f32[2,128,128]{2,1,0:T(8,128)}, u32[]{:S(2)}) copy-start(f32[2,128,128]{2,1,0:T(8,128)} %param.17) | copy-start | bytes 393220
  9.0 33.3 %all-to-all-start = ((f32[64,1,2]{2,1,0:T(1,128)}), f32[64,1,2]{2,1,0:T(1,128)S(1)}, u32[]{:S(2)}, u32[]{:S(2)}) async-start(f32[64,1,2]{2,1,0:T(1,128)} %broadcast_in_dim.57), calls=%async_computation | async-start | bytes 65536 | tf_op jit(solution)/shard_map/all_to_all | solution.py:49
  42.3 8.0 %all-to-all-start.1 = ((f32[8,2,128]{2,1,0:T(2,128)}), f32[8,2,128]{2,1,0:T(2,128)S(1)}, u32[]{:S(2)}, u32[]{:S(2)}) async-start(f32[8,2,128]{2,1,0:T(2,128)} %bitcast.5), calls=%async_computation.1 | async-start | bytes 16384 | tf_op jit(solution)/shard_map/all_to_all | solution.py:43
  47.1 104.6 %all-gather.7.cloned.1.call-start = ((), (), s32[]{:S(2)}) async-start(), calls=%async_computation.2 | async-start | bytes 2228224 | tf_op jit(solution)/shard_map/all_gather | solution.py:25
  74.1 13.9 %copy-start.5 = (f32[2,2,128,128]{2,3,0,1:T(8,128)}, f32[2,2,128,128]{2,3,0,1:T(8,128)S(1)}, u32[]{:S(2)}) copy-start(f32[2,2,128,128]{2,3,0,1:T(8,128)S(1)} %get-tuple-element.45) | copy-start | bytes 786436
  74.1 29.7 %copy-start.7 = (f32[2,2,128,128]{3,2,0,1:T(8,128)}, f32[2,2,128,128]{3,2,0,1:T(8,128)S(1)}, u32[]{:S(2)}) copy-start(f32[2,2,128,128]{3,2,0,1:T(8,128)S(1)} %get-tuple-element.44) | copy-start | bytes 786436
  74.1 15.5 %copy-start.9 = (bf16[128,2,128]{2,1,0:T(2,128)(2,1)S(1)}, bf16[128,2,128]{2,1,0:T(2,128)(2,1)}, u32[]{:S(2)}) copy-start(bf16[128,2,128]{2,1,0:T(2,128)(2,1)} %param.10) | copy-start | bytes 196612
  89.5 134.4 %all-gather.9.cloned.1.call-start = ((), (), s32[]{:S(2)}) async-start(), calls=%async_computation.3 | async-start | bytes 2228224 | tf_op jit(solution)/shard_map/all_gather | solution.py:25
  89.8 15.8 %copy-start.4 = (f32[2,128,128]{2,1,0:T(8,128)S(1)}, f32[2,128,128]{2,1,0:T(8,128)}, u32[]{:S(2)}) copy-start(f32[2,128,128]{2,1,0:T(8,128)} %fusion.91) | copy-start | bytes 393220
  151.7 4.9 %copy-start.1 = (f32[32,128,128]{2,1,0:T(8,128)S(1)}, f32[32,128,128]{2,1,0:T(8,128)}, u32[]{:S(2)}) copy-start(f32[32,128,128]{2,1,0:T(8,128)} %all-gather.7.cloned.1.call-done) | copy-start | bytes 6291460
  223.9 4.8 %copy-start.2 = (f32[32,128,128]{2,1,0:T(8,128)S(1)}, f32[32,128,128]{2,1,0:T(8,128)}, u32[]{:S(2)}) copy-start(f32[32,128,128]{2,1,0:T(8,128)} %all-gather.9.cloned.1.call-done) | copy-start | bytes 6291460
  231.5 1.2 copy-start.3
  231.8 1.2 copy-start.6
  231.8 1.2 copy-start.8
  232.7 3.3 %copy-start.10 = (bf16[128,2,128]{2,1,0:T(2,128)(2,1)S(1)}, bf16[128,2,128]{2,1,0:T(2,128)(2,1)}, u32[]{:S(2)}) copy-start(bf16[128,2,128]{2,1,0:T(2,128)(2,1)} %param.13) | copy-start | bytes 196612
Sparse Core Ops, SparseCore 0:
  89.6 62.1 all-gather.6
  153.8 70.0 all-gather.8
where the time goes:
time: 244 us
  waiting for transfers between devices  122 us (50%)
  matrix products  28.1 us (12%)
  blocking collectives  27 us (11%)
  other arithmetic  24.3 us (10%)
  starting transfers between devices  23.6 us (10%)
  between operations  14.7 us (6%)
  local copies, waits for them, and re-layouts  3.81 us (2%)
    all_gather x2, waiting for transfers between devices, entering(): pieces = jax.tree.map(lambda part: lax.all_gather(part, axis), so_far)  110 us
    all_gather x2, blocking collectives, entering(): pieces = jax.tree.map(lambda part: lax.all_gather(part, axis), so_far)  27 us
    dot_general x53, matrix products, matmul(): jnp.einsum('...ij,...jk->...ik', matrix, operand, precision=lax.Precision...  24 us
    another operation x4, other arithmetic, block_parts(): lax.linalg.triangular_solve(system, right_side, left_side=True, lower=Tru...  19.8 us
    all_to_all x1, starting transfers between devices, from_everyone(): return lax.all_to_all(copies, axis, split_axis=0, concat_axis=0, tiled=True)  18.7 us
    all_to_all x1, waiting for transfers between devices, from_everyone(): return lax.all_to_all(copies, axis, split_axis=0, concat_axis=0, tiled=True)  10.5 us
  transfers between devices with their start and end apart: 4, of which 4 were waited for; matrix products, arithmetic and copies ran while one was open for 7% of the time, Pallas kernels for 0%

commit v1 on v0

v1 whole, which is shorter than its diff:
```python
import functools

import jax
import jax.numpy as jnp
from jax import lax
from jax.experimental import pallas as pl
from jax.experimental.pallas import tpu as pltpu
from jax.sharding import PartitionSpec as P

MESH = pl.DeviceIdType.MESH
F32 = jnp.float32
BF16 = jnp.bfloat16
EPSILON = 1e-06
Y = 4
Z4 = 4
TOK = 128
HALF = 64
DIM = 128
SL = DIM // Y
NH = 2

NN = (((1,), (0,)), ((), ()))
NT = (((1,), (1,)), ((), ()))


def bdot(a, b, dims):
    return lax.dot_general(a, b, dims, preferred_element_type=F32)


def split(x):
    high = x.astype(BF16)
    return high, (x - high.astype(F32)).astype(BF16)


def mm(a, b, dims=NN):
    ah, al = split(a)
    bh, bl = split(b)
    return bdot(ah, bh, dims) + (bdot(al, bh, dims) + bdot(ah, bl, dims))


def mm_right_exact(a, b, dims=NN):
    ah, al = split(a)
    return bdot(ah, b, dims) + bdot(al, b, dims)


def mm_left_exact(a, b, dims=NN):
    bh, bl = split(b)
    return bdot(a, bh, dims) + bdot(a, bl, dims)


def unit_lower_inverse(strict_part, row, col, eye):
    def same(size):
        return (row // size) == (col // size)

    base = jnp.where(same(8), strict_part, 0.0)
    square = mm(base, base)
    cube = mm(base, square)
    fourth = mm(square, square)
    part = eye - base + square - cube
    inverse = part + mm(part, fourth)
    size = 8
    while size < TOK:
        below = jnp.where(same(2 * size) & jnp.logical_not(same(size)), strict_part, 0.0)
        inverse = inverse - mm(inverse, mm(below, inverse))
        size *= 2
    return inverse


def kernel(
    n_seq,
    n_head,
    q_ref,
    k_ref,
    v_ref,
    gate_ref,
    x_ref,
    w_ref,
    ld_ref,
    s0_ref,
    out_ref,
    st_ref,
    lg,
    lg_in,
    kt,
    kty_in,
    ktz,
    ktz_in,
    ta,
    oa,
    oown,
    et,
    eo,
    b1t,
    b1o,
    b2t,
    b2o,
    pt,
    po,
    p4t,
    p4o,
    ext,
    exo,
    seg_s,
    nxt,
    sd,
    sin,
    s0t,
    r_s,
    c_s,
    t0_s,
    o0_s,
    lg_send,
    lg_recv,
    kty_send,
    kty_recv,
    ktz_send,
    ktz_recv,
    a_send,
    a_recv,
    f_send,
    oa_send,
    oa_recv,
    b_send,
    b_recv,
    seg_send,
    seg_recv,
    sd_send,
    sd_recv,
):
    nz = n_seq // Y
    nseg = nz // Z4
    s = lax.axis_index("seq")
    h = lax.axis_index("head")
    z = s // Y
    y = s % Y
    zl = z % Z4
    seg = z // Z4

    def at_y(d):
        return {"seq": z * Y + (y + d) % Y, "head": h}

    def at_z(d):
        return {"seq": ((z + d) % nz) * Y + y, "head": h}

    def at_head(d):
        return {"seq": s, "head": (h + d) % n_head}

    def rcopy(src, dst, ssem, rsem, dev):
        return pltpu.make_async_remote_copy(
            src_ref=src, dst_ref=dst, send_sem=ssem, recv_sem=rsem, device_id=dev, device_id_type=MESH
        )

    barrier = pltpu.get_barrier_semaphore()
    partners = (
        [at_head(d) for d in range(1, n_head)]
        + [at_y(d) for d in range(1, Y)]
        + [at_z(d) for d in range(1, nz)]
    )
    for dev in partners:
        pl.semaphore_signal(barrier, inc=1, device_id=dev, device_id_type=MESH)

    logits = bdot(w_ref[...], x_ref[...], NT)
    for p in range(n_head):
        lg[p] = logits[NH * p : NH * p + NH]
    ks = [k_ref[:, i, :] for i in range(NH)]
    qs = [q_ref[:, i, :] for i in range(NH)]
    vs = [v_ref[:, i, :] for i in range(NH)]
    ksq = [jnp.sum(jnp.square(k.astype(F32)), axis=1, keepdims=True) for k in ks]
    qsq = [jnp.sum(jnp.square(q.astype(F32)), axis=1, keepdims=True) for q in qs]
    tot = [jnp.sum(a, axis=0, keepdims=True) for a in ksq]
    sub = lax.broadcasted_iota(jnp.int32, (8, 128), 0)
    kt[...] = jnp.where(sub == 0, tot[0], jnp.where(sub == 1, tot[1], 0.0))

    pl.semaphore_wait(barrier, len(partners))

    kty = [rcopy(kt, kty_in.at[d], kty_send.at[d], kty_recv.at[d], at_y(d)) for d in range(1, Y)]
    for c in kty:
        c.start()
    lgc = [
        rcopy(lg.at[(h + d) % n_head], lg_in.at[d], lg_send.at[d], lg_recv.at[d], at_head(d))
        for d in range(1, n_head)
    ]
    for c in lgc:
        c.start()

    row = lax.broadcasted_iota(jnp.int32, (TOK, TOK), 0)
    col = lax.broadcasted_iota(jnp.int32, (TOK, TOK), 1)
    low = row >= col
    strict = row > col
    eye = jnp.where(row == col, 1.0, 0.0)
    lane = lax.broadcasted_iota(jnp.int32, (1, TOK), 1)

    def to_row(column):
        return jnp.sum(jnp.where(row == col, column, 0.0), axis=0, keepdims=True)

    gram, score, damp, gcol, grow, ktr, vtr = [], [], [], [], [], [], []
    for i in range(NH):
        gram.append(bdot(ks[i], ks[i], NT))
        score.append(bdot(qs[i], ks[i], NT))
        decay = ld_ref[i : i + 1, :]
        gc = jnp.sum(jnp.where(low, decay, 0.0), axis=1, keepdims=True)
        gr = to_row(gc)
        gcol.append(gc)
        grow.append(gr)
        damp.append(jnp.where(low, jnp.exp(jnp.where(low, gc - gr, 0.0)), 0.0))
        ktr.append(ks[i].T)
        vtr.append(vs[i].T)

    for c in kty:
        c.wait_recv()
    total_y = kt[...]
    for d in range(1, Y):
        total_y = total_y + kty_in[d]
    ktz[...] = total_y
    ktzc = [rcopy(ktz, ktz_in.at[d], ktz_send.at[d], ktz_recv.at[d], at_z(d)) for d in range(1, nz)]
    for c in ktzc:
        c.start()

    for c in lgc:
        c.wait_recv()
    logit = lg[h]
    for d in range(1, n_head):
        logit = logit + lg_in[d]
    beta = 1.0 / (1.0 + jnp.exp(-logit))
    brow = [beta[i : i + 1, :] for i in range(NH)]
    bcol = [jnp.sum(jnp.where(row == col, b, 0.0), axis=1, keepdims=True) for b in brow]

    for c in ktzc:
        c.wait_recv()
    total = ktz[...]
    for d in range(1, nz):
        total = total + ktz_in[d]
    limit = jnp.sqrt(total / float(n_seq * TOK) + EPSILON)

    wr_t, ur_t, rkc, rkr = [], [], [], []
    for i in range(NH):
        rc = 1.0 / jnp.maximum(jnp.sqrt(ksq[i]), limit[i : i + 1, 0:1])
        rr = to_row(rc)
        rkc.append(rc)
        rkr.append(rr)
        a = jnp.where(strict, gram[i] * damp[i] * (bcol[i] * rc) * rr, 0.0)
        inv = unit_lower_inverse(a, row, col, eye)
        wr_t.append(mm_left_exact(ktr[i], inv * (brow[i] * jnp.exp(grow[i]) * rr), NT))
        ur_t.append(mm_left_exact(vtr[i], inv * brow[i], NT))
        glast = grow[i][:, TOK - 1 : TOK]
        crow = rr * jnp.exp(glast - grow[i])
        ta[y, i] = jnp.exp(glast) * eye - mm_right_exact(wr_t[i] * crow, ks[i])
        oown[i] = mm_right_exact(ur_t[i] * crow, ks[i])

    ac = []
    for i in range(NH):
        for j, d in enumerate((1, 3)):
            hh = i if j == 0 else 1 - i
            c = rcopy(ta.at[y, hh], ta.at[y, hh], a_send.at[2 * i + j], a_recv.at[y, hh], at_y(d))
            c.start()
            ac.append(c)
    oc = []
    for d in range(1, Y):
        c = rcopy(
            oown.at[:, pl.ds(pl.multiple_of(((y + d) % Y) * SL, SL), SL), :],
            oa.at[y],
            oa_send.at[d],
            oa_recv.at[y],
            at_y(d),
        )
        c.start()
        oc.append(c)
    oa[y] = oown[:, pl.ds(pl.multiple_of(y * SL, SL), SL), :]

    left, right = (y + 3) % Y, (y + 1) % Y
    far = (y + 2) % Y

    def arrived_a(slot, hh):
        rcopy(ta.at[slot, hh], ta.at[slot, hh], a_send.at[0], a_recv.at[slot, hh], at_y(1)).wait_recv()

    arrived_a(left, 0)
    f0 = rcopy(ta.at[left, 0], ta.at[left, 0], f_send.at[0], a_recv.at[left, 0], at_y(1))
    f0.start()
    arrived_a(right, 1)
    f1 = rcopy(ta.at[right, 1], ta.at[right, 1], f_send.at[1], a_recv.at[right, 1], at_y(3))
    f1.start()

    for i in range(NH):
        rq = float(DIM) ** (-0.5) / jnp.sqrt(qsq[i] + EPSILON)
        prob = score[i] * damp[i] * rq * rkr[i]
        r_s[i] = qs[i].astype(F32) * (rq * jnp.exp(gcol[i])) - mm(prob, wr_t[i], NT)
        c_s[i] = mm(prob, ur_t[i], NT)
        gmid = grow[i][:, HALF - 1 : HALF]
        crow0 = jnp.where(lane < HALF, rkr[i] * jnp.exp(jnp.where(lane < HALF, gmid - grow[i], 0.0)), 0.0)
        t0_s[i] = jnp.exp(gmid) * eye - mm_left_exact(ktr[i], wr_t[i] * crow0, NT)
        o0_s[i] = mm_left_exact(ktr[i], ur_t[i] * crow0, NT)

    @pl.when(seg == 0)
    def _():
        for i in range(NH):
            s0t[i] = s0_ref[i].T
        seg_s[...] = s0t[:, pl.ds(pl.multiple_of(y * SL, SL), SL), :]

    arrived_a(left, 1)
    arrived_a(right, 0)
    arrived_a(far, 0)
    arrived_a(far, 1)
    for d in range(1, Y):
        slot = (y + Y - d) % Y
        rcopy(oa.at[slot], oa.at[slot], oa_send.at[0], oa_recv.at[slot], at_y(1)).wait_recv()

    for i in range(NH):
        mt, mo = ta[0, i], oa[0, i]
        et[0, i] = mt
        eo[0, i] = mo
        for k in range(1, Y):
            step = ta[k, i]
            mt, mo = mm(mt, step), mm(mo, step) + oa[k, i]
            et[k, i] = mt
            eo[k, i] = mo
    gt, go = et.at[Y - 1], eo.at[Y - 1]

    def to_b1():
        return [
            rcopy(gt, b1t, b_send.at[0], b_recv.at[0], at_z(1)),
            rcopy(go, b1o, b_send.at[1], b_recv.at[1], at_z(1)),
        ]

    def to_b2(d):
        return [
            rcopy(pt, b2t, b_send.at[2 * d], b_recv.at[2], at_z(d)),
            rcopy(po, b2o, b_send.at[2 * d + 1], b_recv.at[3], at_z(d)),
        ]

    def then(first, second, out):
        for i in range(NH):
            step = second[0][i]
            out[0][i] = mm(first[0][i], step)
            out[1][i] = mm(first[1][i], step) + second[1][i]

    @pl.when(zl % 2 == 0)
    def _():
        for c in to_b1():
            c.start()

    @pl.when(zl % 2 == 1)
    def _():
        for c in to_b1():
            c.wait_recv()
        then((b1t, b1o), (gt, go), (pt, po))

    @pl.when(zl == 1)
    def _():
        for d in (2, 1):
            for c in to_b2(d):
                c.start()

    @pl.when(zl >= 2)
    def _():
        for c in to_b2(1):
            c.wait_recv()

    @pl.when(zl == 3)
    def _():
        then((b2t, b2o), (pt, po), (p4t, p4o))

    def to_seg(d):
        return rcopy(nxt, seg_s, seg_send.at[d], seg_recv, at_z(d))

    @pl.when(seg > 0)
    def _():
        to_seg(1).wait_recv()

    @pl.when((zl == 3) & (seg < nseg - 1))
    def _():
        for i in range(NH):
            nxt[i] = mm(seg_s[i], p4t[i]) + p4o[i]
        for d in (4, 3, 2, 1):
            to_seg(d).start()

    @pl.when(zl == 3)
    def _():
        then((b2t, b2o), (b1t, b1o), (ext, exo))

    @pl.when(zl == 0)
    def _():
        sd[0] = seg_s[...]

    @pl.when(zl == 1)
    def _():
        for i in range(NH):
            sd[0, i] = mm(seg_s[i], b1t[i]) + b1o[i]

    @pl.when(zl == 2)
    def _():
        for i in range(NH):
            sd[0, i] = mm(seg_s[i], b2t[i]) + b2o[i]

    @pl.when(zl == 3)
    def _():
        for i in range(NH):
            sd[0, i] = mm(seg_s[i], ext[i]) + exo[i]

    for k in range(1, Y):
        for i in range(NH):
            sd[k, i] = mm(sd[0, i], et[k - 1, i]) + eo[k - 1, i]

    mine = pl.ds(pl.multiple_of(y * SL, SL), SL)
    sdc = [
        rcopy(sd.at[(y + d) % Y], sin.at[:, mine, :], sd_send.at[d], sd_recv.at[d], at_y(d))
        for d in range(1, Y)
    ]
    for c in sdc:
        c.start()
    sin[:, mine, :] = sd[y]
    for c in sdc:
        c.wait_recv()

    for i in range(NH):
        state_t = sin[i]
        raw = mm(r_s[i], state_t, NT) + c_s[i]
        inverse_rms = 1.0 / jnp.sqrt(jnp.mean(raw * raw, axis=1, keepdims=True) + EPSILON)
        gate = gate_ref[:, i, :].astype(F32)
        out_ref[i] = (raw * inverse_rms * (gate / (1.0 + jnp.exp(-gate)))).astype(BF16)
        st_ref[0, i] = state_t.T
        st_ref[1, i] = mm(t0_s[i], state_t, NT) + o0_s[i]

    for c in kty + lgc + ktzc + ac + oc + [f0, f1] + sdc:
        c.wait_send()

    @pl.when(zl % 2 == 0)
    def _():
        for c in to_b1():
            c.wait_send()

    @pl.when(zl == 1)
    def _():
        for d in (2, 1):
            for c in to_b2(d):
                c.wait_send()

    @pl.when((zl == 3) & (seg < nseg - 1))
    def _():
        for d in (4, 3, 2, 1):
            to_seg(d).wait_send()


def on_device(n_seq, n_head, queries, key_vectors, values, out_gate, inputs, beta_weight, log_decay, initial_state):
    nz = n_seq // Y
    vm = pl.BlockSpec(memory_space=pltpu.VMEM)
    full = pltpu.VMEM((NH, DIM, DIM), F32)
    slim = pltpu.VMEM((NH, SL, DIM), F32)
    dma = pltpu.SemaphoreType.DMA
    out, states = pl.pallas_call(
        functools.partial(kernel, n_seq, n_head),
        out_shape=(
            jax.ShapeDtypeStruct((NH, TOK, DIM), BF16),
            jax.ShapeDtypeStruct((2, NH, DIM, DIM), F32),
        ),
        in_specs=[vm] * 8,
        out_specs=(vm, vm),
        scratch_shapes=[
            pltpu.VMEM((n_head, NH, TOK), F32),
            pltpu.VMEM((n_head, NH, TOK), F32),
            pltpu.VMEM((8, 128), F32),
            pltpu.VMEM((Y, 8, 128), F32),
            pltpu.VMEM((8, 128), F32),
            pltpu.VMEM((nz, 8, 128), F32),
            pltpu.VMEM((Y, NH, DIM, DIM), F32),
            pltpu.VMEM((Y, NH, SL, DIM), F32),
            full,
            pltpu.VMEM((Y, NH, DIM, DIM), F32),
            pltpu.VMEM((Y, NH, SL, DIM), F32),
            full,
            slim,
            full,
            slim,
            full,
            slim,
            full,
            slim,
            full,
            slim,
            slim,
            slim,
            pltpu.VMEM((Y, NH, SL, DIM), F32),
            full,
            full,
            full,
            full,
            full,
            full,
            dma((n_head,)),
            dma((n_head,)),
            dma((Y,)),
            dma((Y,)),
            dma((nz,)),
            dma((nz,)),
            dma((4,)),
            dma((Y, NH)),
            dma((2,)),
            dma((Y,)),
            dma((Y,)),
            dma((6,)),
            dma((4,)),
            dma((5,)),
            dma(()),
            dma((Y,)),
            dma((Y,)),
        ],
        compiler_params=pltpu.CompilerParams(collective_id=0, has_side_effects=True),
        name="delta_layer",
    )(queries, key_vectors, values, out_gate, inputs, beta_weight, log_decay, initial_state)
    return out.transpose(1, 0, 2), states


def solution(mesh):
    in_specs = (
        P("seq", "head", None),
        P("seq", "head", None),
        P("seq", "head", None),
        P("seq", "head", None),
        P("seq", "head"),
        P(None, "head"),
        P("head", "seq"),
        P("head", None, None),
    )
    out_specs = (P("seq", "head", None), P("seq", "head", None, None))
    body = functools.partial(on_device, mesh.shape["seq"], mesh.shape["head"])
    return jax.shard_map(body, mesh=mesh, in_specs=in_specs, out_specs=out_specs, check_vma=False)
```

time: 244 us -> 68.3 us (0.28)
  the two profiles are of different devices: /device:TPU:6 before, /device:TPU:482 now
where the time goes in v1:
time: 68.3 us; the launch traced here: 68.1 us
  Pallas kernels  64.3 us (94%)
  local copies, waits for them, and re-layouts  3.21 us (5%)
    pallas_call x1, Pallas kernels, on_device(): pl.pallas_call(functools.partial(kernel, n_seq, n_head), out_shape=(jax.S...  64.3 us
    unnamed x2, local copies, waits for them, and re-layouts  3.21 us

profile of v1, /device:TPU:482, one launch (start us, length us, event | category | flops | bytes accessed | tf_op | source)
XLA Modules:
  0.0 68.1 jit_solution(18061127250968329239)
XLA Ops:
  0.6 64.3 %delta_layer.1 = (bf16[2,128,128]{2,1,0:T(8,128)(2,1)}, f32[2,2,128,128]{3,2,1,0:T(8,128)}) custom-call(bf16[128,2,128]{2,1,0:T(2,128)(2,1)} %q_ref.1, bf16[128,2,128]{2,1,0:T(2,128)(2,1)} %k_ref.1, bf16[128,2,128]{2,1,0:T(2,128)(2,1)} %v_ref.1, bf16[128,2,128]{2,1,0:T(2,128)(2,1)} %gate_ref.1, bf16[128,256]{1,0:T(8,128)(2,1)} %x_ref.1, ...), custom_call_target="tpu_custom_call" | custom-call | tf_op jit(solution)/shard_map/delta_layer/pallas_call | solution.py:449
  64.9 1.5 %copy.10 = bf16[128,2,128]{2,1,0:T(2,128)(2,1)} copy(bf16[128,2,128]{2,0,1:T(8,128)(2,1)} %bitcast.1) | data formatting | bytes 131072
  66.5 1.7 %copy.12 = f32[2,2,128,128]{3,2,1,0:T(8,128)} copy(f32[2,2,128,128]{3,2,1,0:T(8,128)} %get-tuple-element.11) | data formatting | bytes 524288

commit v2 on v1

--- a/solution.py
+++ b/solution.py
@@ -72,13 +72,15 @@
     q_ref,
     k_ref,
     v_ref,
-    gate_ref,
     x_ref,
     w_ref,
     ld_ref,
     s0_ref,
-    out_ref,
-    st_ref,
+    start_s,
+    r_s,
+    c_s,
+    t0_s,
+    o0_s,
     lg,
     lg_in,
     kt,
@@ -105,10 +107,6 @@
     sd,
     sin,
     s0t,
-    r_s,
-    c_s,
-    t0_s,
-    o0_s,
     lg_send,
     lg_recv,
     kty_send,
@@ -290,7 +288,7 @@
         t0_s[i] = jnp.exp(gmid) * eye - mm_left_exact(ktr[i], wr_t[i] * crow0, NT)
         o0_s[i] = mm_left_exact(ktr[i], ur_t[i] * crow0, NT)
 
-    @pl.when(seg == 0)
+    @pl.when(z == 0)
     def _():
         for i in range(NH):
             s0t[i] = s0_ref[i].T
@@ -314,87 +312,128 @@
             et[k, i] = mt
             eo[k, i] = mo
     gt, go = et.at[Y - 1], eo.at[Y - 1]
-
-    def to_b1():
+    first = seg == 0
+
+    def to_b1(i):
         return [
-            rcopy(gt, b1t, b_send.at[0], b_recv.at[0], at_z(1)),
-            rcopy(go, b1o, b_send.at[1], b_recv.at[1], at_z(1)),
+            rcopy(gt.at[i], b1t.at[i], b_send.at[2 * i], b_recv.at[2 * i], at_z(1)),
+            rcopy(go.at[i], b1o.at[i], b_send.at[2 * i + 1], b_recv.at[2 * i + 1], at_z(1)),
         ]
 
-    def to_b2(d):
+    def to_b2(d, i):
+        k = 4 * d + 2 * i
         return [
-            rcopy(pt, b2t, b_send.at[2 * d], b_recv.at[2], at_z(d)),
-            rcopy(po, b2o, b_send.at[2 * d + 1], b_recv.at[3], at_z(d)),
+            rcopy(pt.at[i], b2t.at[i], b_send.at[k], b_recv.at[4 + 2 * i], at_z(d)),
+            rcopy(po.at[i], b2o.at[i], b_send.at[k + 1], b_recv.at[5 + 2 * i], at_z(d)),
         ]
 
-    def then(first, second, out):
-        for i in range(NH):
-            step = second[0][i]
-            out[0][i] = mm(first[0][i], step)
-            out[1][i] = mm(first[1][i], step) + second[1][i]
-
-    @pl.when(zl % 2 == 0)
-    def _():
-        for c in to_b1():
-            c.start()
-
-    @pl.when(zl % 2 == 1)
-    def _():
-        for c in to_b1():
-            c.wait_recv()
-        then((b1t, b1o), (gt, go), (pt, po))
-
-    @pl.when(zl == 1)
-    def _():
+    def then(first_map, second_map, out, i):
+        step = second_map[0][i]
+        out[0][i] = mm(first_map[0][i], step)
+        out[1][i] = mm(first_map[1][i], step) + second_map[1][i]
+
+    def apply(state, by, out, i):
+        out[i] = mm(state[i], by[0][i]) + by[1][i]
+
+    sends_b1 = (zl == 2) | ((zl == 0) & (seg > 0))
+    takes_b1 = (zl == 3) | ((zl == 1) & (seg > 0))
+    sends_b2 = (zl == 1) & (seg > 0)
+    takes_b2 = (zl >= 2) & (seg > 0)
+
+    def to_next(d):
+        return rcopy(nxt, seg_s, seg_send.at[d], seg_recv, at_z(d))
+
+    @pl.when(z == 0)
+    def _():
+        for i in range(NH):
+            apply(seg_s, (gt, go), nxt, i)
+        to_next(1).start()
+
+    @pl.when(sends_b1)
+    def _():
+        for i in range(NH):
+            for c in to_b1(i):
+                c.start()
+
+    @pl.when(takes_b1)
+    def _():
+        for i in range(NH):
+            for c in to_b1(i):
+                c.wait_recv()
+            then((b1t, b1o), (gt, go), (pt, po), i)
+
+            @pl.when(sends_b2)
+            def _(i=i):
+                for c in to_b2(2, i):
+                    c.start()
+
+    @pl.when(sends_b2)
+    def _():
+        for i in range(NH):
+            for c in to_b2(1, i):
+                c.start()
+
+    @pl.when(takes_b2)
+    def _():
+        for i in range(NH):
+            for c in to_b2(1, i):
+                c.wait_recv()
+
+    @pl.when((zl == 3) & (seg > 0))
+    def _():
+        for i in range(NH):
+            then((b2t, b2o), (pt, po), (p4t, p4o), i)
+        for i in range(NH):
+            then((b2t, b2o), (b1t, b1o), (ext, exo), i)
+
+    @pl.when(z > 0)
+    def _():
+        to_next(1).wait_recv()
+
+    @pl.when(z == 1)
+    def _():
+        for i in range(NH):
+            apply(seg_s, (gt, go), nxt, i)
         for d in (2, 1):
-            for c in to_b2(d):
-                c.start()
-
-    @pl.when(zl >= 2)
-    def _():
-        for c in to_b2(1):
-            c.wait_recv()
-
-    @pl.when(zl == 3)
-    def _():
-        then((b2t, b2o), (pt, po), (p4t, p4o))
-
-    def to_seg(d):
-        return rcopy(nxt, seg_s, seg_send.at[d], seg_recv, at_z(d))
-
-    @pl.when(seg > 0)
-    def _():
-        to_seg(1).wait_recv()
-
-    @pl.when((zl == 3) & (seg < nseg - 1))
-    def _():
-        for i in range(NH):
-            nxt[i] = mm(seg_s[i], p4t[i]) + p4o[i]
-        for d in (4, 3, 2, 1):
-            to_seg(d).start()
-
-    @pl.when(zl == 3)
-    def _():
-        then((b2t, b2o), (b1t, b1o), (ext, exo))
-
-    @pl.when(zl == 0)
+            to_next(d).start()
+
+    if nseg > 1:
+
+        @pl.when(z == 3)
+        def _():
+            for i in range(NH):
+                apply(seg_s, (pt, po), nxt, i)
+
+        @pl.when((zl == 3) & (seg > 0) & (seg < nseg - 1))
+        def _():
+            for i in range(NH):
+                apply(seg_s, (p4t, p4o), nxt, i)
+
+        @pl.when((zl == 3) & (seg < nseg - 1))
+        def _():
+            for d in (4, 3, 2, 1):
+                to_next(d).start()
+
+    start = sd.at[0]
+
+    @pl.when((zl == 0) | (first & (zl < 3)))
     def _():
         sd[0] = seg_s[...]
 
-    @pl.when(zl == 1)
-    def _():
-        for i in range(NH):
-            sd[0, i] = mm(seg_s[i], b1t[i]) + b1o[i]
-
-    @pl.when(zl == 2)
-    def _():
-        for i in range(NH):
-            sd[0, i] = mm(seg_s[i], b2t[i]) + b2o[i]
-
-    @pl.when(zl == 3)
-    def _():
-        for i in range(NH):
-            sd[0, i] = mm(seg_s[i], ext[i]) + exo[i]
+    @pl.when(sends_b2 | (z == 3))
+    def _():
+        for i in range(NH):
+            apply(seg_s, (b1t, b1o), start, i)
+
+    @pl.when((zl == 2) & (seg > 0))
+    def _():
+        for i in range(NH):
+            apply(seg_s, (b2t, b2o), start, i)
+
+    @pl.when((zl == 3) & (seg > 0))
+    def _():
+        for i in range(NH):
+            apply(seg_s, (ext, exo), start, i)
 
     for k in range(1, Y):
         for i in range(NH):
@@ -410,34 +449,53 @@
     sin[:, mine, :] = sd[y]
     for c in sdc:
         c.wait_recv()
-
+    start_s[...] = sin[...]
+
+    for c in kty + lgc + ktzc + ac + oc + [f0, f1] + sdc:
+        c.wait_send()
+
+    @pl.when(sends_b1)
+    def _():
+        for i in range(NH):
+            for c in to_b1(i):
+                c.wait_send()
+
+    @pl.when(sends_b2)
+    def _():
+        for d in (2, 1):
+            for i in range(NH):
+                for c in to_b2(d, i):
+                    c.wait_send()
+
+    @pl.when(z == 0)
+    def _():
+        to_next(1).wait_send()
+
+    @pl.when(z == 1)
+    def _():
+        for d in (2, 1):
+            to_next(d).wait_send()
+
+    if nseg > 1:
+
+        @pl.when((zl == 3) & (seg < nseg - 1))
+        def _():
+            for d in (4, 3, 2, 1):
+                to_next(d).wait_send()
+
+
+def finish(gate_ref, sin, r_s, c_s, t0_s, o0_s, out_ref, st_ref):
+    gated = []
     for i in range(NH):
         state_t = sin[i]
         raw = mm(r_s[i], state_t, NT) + c_s[i]
         inverse_rms = 1.0 / jnp.sqrt(jnp.mean(raw * raw, axis=1, keepdims=True) + EPSILON)
         gate = gate_ref[:, i, :].astype(F32)
-        out_ref[i] = (raw * inverse_rms * (gate / (1.0 + jnp.exp(-gate)))).astype(BF16)
+        gated.append(raw * inverse_rms * (gate / (1.0 + jnp.exp(-gate))))
         st_ref[0, i] = state_t.T
         st_ref[1, i] = mm(t0_s[i], state_t, NT) + o0_s[i]
-
-    for c in kty + lgc + ktzc + ac + oc + [f0, f1] + sdc:
-        c.wait_send()
-
-    @pl.when(zl % 2 == 0)
-    def _():
-        for c in to_b1():
-            c.wait_send()
-
-    @pl.when(zl == 1)
-    def _():
-        for d in (2, 1):
-            for c in to_b2(d):
-                c.wait_send()
-
-    @pl.when((zl == 3) & (seg < nseg - 1))
-    def _():
-        for d in (4, 3, 2, 1):
-            to_seg(d).wait_send()
+    for i in range(NH):
+        out_ref[:, i, :] = gated[i].astype(BF16)
 
 
 def on_device(n_seq, n_head, queries, key_vectors, values, out_gate, inputs, beta_weight, log_decay, initial_state):
@@ -446,14 +504,11 @@
     full = pltpu.VMEM((NH, DIM, DIM), F32)
     slim = pltpu.VMEM((NH, SL, DIM), F32)
     dma = pltpu.SemaphoreType.DMA
-    out, states = pl.pallas_call(
+    parts = pl.pallas_call(
         functools.partial(kernel, n_seq, n_head),
-        out_shape=(
-            jax.ShapeDtypeStruct((NH, TOK, DIM), BF16),
-            jax.ShapeDtypeStruct((2, NH, DIM, DIM), F32),
-        ),
-        in_specs=[vm] * 8,
-        out_specs=(vm, vm),
+        out_shape=[full] * 5,
+        in_specs=[vm] * 7,
+        out_specs=[vm] * 5,
         scratch_shapes=[
             pltpu.VMEM((n_head, NH, TOK), F32),
             pltpu.VMEM((n_head, NH, TOK), F32),
@@ -479,10 +534,6 @@
             slim,
             slim,
             pltpu.VMEM((Y, NH, SL, DIM), F32),
-            full,
-            full,
-            full,
-            full,
             full,
             full,
             dma((n_head,)),
@@ -496,8 +547,8 @@
             dma((2,)),
             dma((Y,)),
             dma((Y,)),
-            dma((6,)),
-            dma((4,)),
+            dma((12,)),
+            dma((8,)),
             dma((5,)),
             dma(()),
             dma((Y,)),
@@ -505,8 +556,17 @@
         ],
         compiler_params=pltpu.CompilerParams(collective_id=0, has_side_effects=True),
         name="delta_layer",
-    )(queries, key_vectors, values, out_gate, inputs, beta_weight, log_decay, initial_state)
-    return out.transpose(1, 0, 2), states
+    )(queries, key_vectors, values, inputs, beta_weight, log_decay, initial_state)
+    return pl.pallas_call(
+        finish,
+        out_shape=(
+            jax.ShapeDtypeStruct((TOK, NH, DIM), BF16),
+            jax.ShapeDtypeStruct((2, NH, DIM, DIM), F32),
+        ),
+        in_specs=[vm] * 6,
+        out_specs=(vm, vm),
+        name="delta_output",
+    )(out_gate, *[pltpu.with_memory_space_constraint(a, pltpu.VMEM) for a in parts])
 
 
 def solution(mesh):

time: 68.3 us -> 62.9 us (0.921)
  local copies, waits for them, and re-layouts: 3.21 us -> 0 us
  Pallas kernels: 64.3 us -> 62.1 us
    unnamed x2 -> x0, local copies, waits for them, and re-layouts: 3.21 us -> none
    pallas_call x1 -> x2, Pallas kernels: 64.3 us -> 62.1 us  [the longest x1 59.7 us: on_device(): pl.pallas_call(functools.partial(kernel, n_seq, n_head), out_shape=[full]...]
where the time goes in v2:
time: 62.9 us; the launch traced here: 62.7 us
  Pallas kernels  62.1 us (99%)
  between operations  0.64 us (1%)
    pallas_call x1, Pallas kernels, on_device(): pl.pallas_call(functools.partial(kernel, n_seq, n_head), out_shape=[full]...  59.7 us
    pallas_call x1, Pallas kernels, on_device(): pl.pallas_call(finish, out_shape=(jax.ShapeDtypeStruct((TOK, NH, DIM), BF...  2.34 us

profile of v2, /device:TPU:482, one launch (start us, length us, event | category | flops | bytes accessed | tf_op | source)
XLA Modules:
  0.0 62.7 jit_solution(671635135578784406)
XLA Ops:
  0.6 59.7 %delta_layer.1 = (f32[2,128,128]{2,1,0:T(8,128)S(1)}, f32[2,128,128]{2,1,0:T(8,128)S(1)}, f32[2,128,128]{2,1,0:T(8,128)S(1)}, f32[2,128,128]{2,1,0:T(8,128)S(1)}, f32[2,128,128]{2,1,0:T(8,128)S(1)}) custom-call(bf16[128,2,128]{2,1,0:T(2,128)(2,1)} %q_ref.1, bf16[128,2,128]{2,1,0:T(2,128)(2,1)} %k_ref.1, bf16[128,2,128]{2,1,0:T(2,128)(2,1)} %v_ref.1, ...), custom_call_target="tpu_custom_call" | custom-call | tf_op jit(solution)/shard_map/delta_layer/pallas_call | solution.py:507
  60.4 2.3 %delta_output.1 = (bf16[128,2,128]{2,1,0:T(2,128)(2,1)}, f32[2,2,128,128]{3,2,1,0:T(8,128)}) custom-call(bf16[128,2,128]{2,1,0:T(2,128)(2,1)} %gate_ref.1, f32[2,128,128]{2,1,0:T(8,128)S(1)} %get-tuple-element.7.sin, f32[2,128,128]{2,1,0:T(8,128)S(1)} %get-tuple-element.8.r_s, f32[2,128,128]{2,1,0:T(8,128)S(1)} %get-tuple-element.9.c_s, ...), custom_call_target="tpu_custom_call" | custom-call | tf_op jit(solution)/shard_map/delta_output/pallas_call | solution.py:560
